TPU v7x, 32 devices: a whole 2x2x4 slice. The times are simulated.
32 devices in a mesh: dap: 32 (over z, y, x, core), ch: 1.
Axes of the slice: x: 2, y: 2, z: 4, core: 2. Of those that a mesh axis runs over, the one named last changes fastest.
Arguments:
- alignment_embedding: bfloat16 [128, 128, 256], P(None, 'dap'), may hold values from -6 to 6
- couple_embedding: bfloat16 [128, 128, 128], P('dap', 'ch'), may hold values from -6 to 6
- tensor_first_matrix: bfloat16 [256, 32], P(None, 'ch'), may hold values from -0.375 to 0.375
- tensor_second_matrix: bfloat16 [256, 32], replicated, may hold values from -0.375 to 0.375
- tensor_final_matrix: bfloat16 [1024, 128], P('ch'), may hold values from -1 to 1
- trimul_entry_matrix: bfloat16 [4, 128, 128], replicated, may hold values from -0.5 to 0.5
- trimul_sigmoid_matrix: bfloat16 [128, 128], replicated, may hold values from -0.5 to 0.5
- trimul_final_matrix: bfloat16 [128, 128], replicated, may hold values from -0.5 to 0.5
Outputs:
- pair_out: bfloat16 [128, 128, 128], P('dap', 'ch')
All inputs are finite; a program needn't handle non-finite values.
Results may differ from a plain program's by a relative error of at most 0.014.
Values may be sent and summed in bfloat16 or wider, within the bound.
A program may use at most 64 MiB of HBM per device.

v0:
```python
import jax
import jax.numpy as jnp
from jax import lax
from jax.sharding import PartitionSpec as P


def standardize_fn(value, axis):
    mean = jnp.mean(value, axis=axis, keepdims=True)
    centred = value - mean
    var = jnp.mean(centred * centred, axis=axis, keepdims=True)
    return centred * lax.rsqrt(var + 1e-05)


def outer_update(first_operand, right_rows, w_out, alignment_height):
    rows = first_operand.shape[1]
    outer = jnp.einsum(
        "sic,sje->ijce", first_operand, right_rows, preferred_element_type=jnp.float32
    )
    outer = (outer * (1.0 / alignment_height)).astype(jnp.bfloat16)
    outer = outer.reshape(rows, right_rows.shape[1], first_operand.shape[2] * right_rows.shape[2])
    return jnp.einsum("ijf,fz->ijz", outer, w_out, preferred_element_type=jnp.float32)


def per_device(
    alignment_embedding,
    couple_embedding,
    tensor_first_matrix,
    tensor_second_matrix,
    tensor_final_matrix,
    trimul_entry_matrix,
    trimul_sigmoid_matrix,
    trimul_final_matrix,
):
    alignment_height = alignment_embedding.shape[0]
    columns = couple_embedding.shape[1]
    alignment_standardized = standardize_fn(alignment_embedding.astype(jnp.float32), -1).astype(
        jnp.bfloat16
    )
    second_operand = jnp.einsum(
        "ziv,vl->zil",
        alignment_standardized,
        tensor_second_matrix,
        preferred_element_type=jnp.float32,
    ).astype(jnp.bfloat16)
    right_all = lax.all_gather(second_operand, "dap", axis=1, tiled=True)
    first_operand = jnp.einsum(
        "ziv,vl->zil",
        alignment_standardized,
        tensor_first_matrix,
        preferred_element_type=jnp.float32,
    ).astype(jnp.bfloat16)
    terms = outer_update(first_operand, right_all, tensor_final_matrix, alignment_height)
    totals = lax.psum(terms.astype(jnp.bfloat16), "ch").astype(jnp.float32)
    update = lax.dynamic_slice_in_dim(totals, lax.axis_index("ch") * columns, columns, 1)
    lifted = (couple_embedding.astype(jnp.float32) + update).astype(jnp.bfloat16)
    normed = standardize_fn(lifted.astype(jnp.float32), -1).astype(jnp.bfloat16)
    projected = jnp.einsum(
        "rkz,qzc->qcrk", normed, trimul_entry_matrix, preferred_element_type=jnp.float32
    )
    left_t = (jax.nn.sigmoid(projected[0]) * projected[1]).astype(jnp.bfloat16)
    right_t = (jax.nn.sigmoid(projected[2]) * projected[3]).astype(jnp.bfloat16)
    left_cols, right_cols = (
        lax.all_to_all(left_t, "dap", split_axis=0, concat_axis=1, tiled=True),
        lax.all_to_all(right_t, "dap", split_axis=0, concat_axis=1, tiled=True),
    )
    product = jnp.einsum("cik,cjk->cij", left_cols, right_cols, preferred_element_type=jnp.float32)
    returned = lax.all_to_all(
        product.astype(jnp.bfloat16), "dap", split_axis=1, concat_axis=0, tiled=True
    ).astype(product.dtype)
    summed = lax.psum_scatter(returned.astype(jnp.bfloat16), "ch", scatter_dimension=2, tiled=True)
    tri_n = standardize_fn(summed.astype(jnp.float32), 0).astype(jnp.bfloat16)
    out = jnp.einsum("crj,cz->rjz", tri_n, trimul_final_matrix, preferred_element_type=jnp.float32)
    gate = jax.nn.sigmoid(
        jnp.einsum("rjz,zy->rjy", normed, trimul_sigmoid_matrix, preferred_element_type=jnp.float32)
    )
    return (lifted.astype(jnp.float32) + gate * out).astype(jnp.bfloat16)


def solution(mesh):
    placed = (
        P(None, "dap", None),
        P("dap", "ch", None),
        P(None, "ch"),
        P(),
        P("ch", None),
        P(),
        P(),
        P(),
    )
    return jax.shard_map(
        per_device, mesh=mesh, in_specs=placed, out_specs=P("dap", "ch", None), check_vma=False
    )
```

profile of v0, /device:TPU:0, one launch (start us, length us, event | category | flops | bytes accessed | tf_op | source)
XLA Modules:
  0.0 114.2 jit_solution(17043596067753059552)
XLA Ops:
  6.5 0.0 copy-start
  6.5 0.0 copy-start.1
  6.5 0.0 copy-start.7
  6.5 0.0 copy-start.2
  6.5 0.0 all-gather.2.cloned.1.call-start
  6.6 1.2 %convert_reduce_fusion = f32[128,4]{1,0:T(8,128)S(1)} fusion(bf16[128,4,256]{2,1,0:T(4,128)(2,1)} %param.8), kind=kLoop, calls=%fused_computation.21 | loop fusion | flops 261632 | bytes 264192 | tf_op jit(solution)/shard_map/reduce_sum | solution.py:8
  7.8 0.0 copy-start.5
  7.8 1.3 %fusion.14 = f32[128,4]{1,0:T(8,128)S(1)} fusion(bf16[128,4,256]{2,1,0:T(4,128)(2,1)} %param.8, f32[128,4]{1,0:T(8,128)S(1)} %broadcast_multiply_fusion), kind=kLoop, calls=%fused_computation.24 | loop fusion | flops 523776 | bytes 266240 | tf_op jit(solution)/shard_map/reduce_sum | solution.py:10
  9.2 0.0 copy-done.1
  9.2 0.3 fusion.15
  9.6 0.0 copy-done.7
  9.6 0.8 convolution_convert_fusion.3
  10.4 0.0 all-gather.2.cloned.1.call-update
  10.4 0.0 copy-done.2
  10.4 0.1 copy.34
  10.5 56.3 %all-gather.2.cloned.1.call-done = bf16[128,128,32]{0,2,1:T(8,128)(2,1)} async-done(((bf16[128,4,32]{0,2,1:T(8,128)(2,1)}), bf16[128,128,32]{0,2,1:T(8,128)(2,1)}) %all-gather.2.cloned.1.call-update) | async-done | bytes 1048592 | tf_op jit(solution)/shard_map/all_gather | solution.py:45
  66.9 0.0 copy-done.5
  66.9 1.9 %fusion = bf16[4,128,32,32]{1,2,0,3:T(8,128)(2,1)S(1)} fusion(bf16[128,128,32,1]{0,2,1,3:T(8,128)(2,1)} %bitcast.65, bf16[128,4,256]{2,1,0:T(4,128)(2,1)S(1)} %fusion.15, bf16[256,32]{0,1:T(8,128)(2,1)S(1)} %copy-done.5), kind=kOutput, calls=%fused_computation.1 | convolution fusion | flops 143671296 | bytes 2375680 | tf_op jit(solution)/shard_map/sic,sje->ijce/dot_general | solution.py:16
  68.8 0.7 copy.38
  69.5 0.0 copy-start.3
  69.5 0.0 copy-done
  69.5 0.4 fusion.41
  69.9 0.5 copy-done.3
  70.4 0.3 convolution_bitcast_fusion
  70.7 0.1 fusion.35
  70.9 0.8 copy.47
  71.6 3.6 %all-to-all-start.1 = ((bf16[128,4,128]{2,1,0:T(4,128)(2,1)}), bf16[128,4,128]{2,1,0:T(4,128)(2,1)S(1)}, u32[]{:S(2)}, u32[]{:S(2)}) async-start(bf16[128,4,128]{2,1,0:T(4,128)(2,1)} %copy.47), calls=%async_computation.1 | async-start | bytes 262144 | tf_op jit(solution)/shard_map/all_to_all | solution.py:64
  75.2 0.8 copy.44
  76.0 7.4 %all-to-all-done.1 = bf16[128,4,128]{2,1,0:T(4,128)(2,1)S(1)} async-done(((bf16[128,4,128]{2,1,0:T(4,128)(2,1)}), bf16[128,4,128]{2,1,0:T(4,128)(2,1)S(1)}, u32[]{:S(2)}, u32[]{:S(2)}) %all-to-all-start.1) | async-done | bytes 131104 | tf_op jit(solution)/shard_map/all_to_all | solution.py:64
  83.4 2.6 %all-to-all-start = ((bf16[128,4,128]{2,1,0:T(4,128)(2,1)}), bf16[128,4,128]{2,1,0:T(4,128)(2,1)S(1)}, u32[]{:S(2)}, u32[]{:S(2)}) async-start(bf16[128,4,128]{2,1,0:T(4,128)(2,1)} %copy.44), calls=%async_computation | async-start | bytes 262144 | tf_op jit(solution)/shard_map/all_to_all | solution.py:63
  86.0 0.0 copy-start.6
  86.1 0.1 copy.49
  86.2 8.1 %all-to-all-done = bf16[128,4,128]{2,1,0:T(4,128)(2,1)S(1)} async-done(((bf16[128,4,128]{2,1,0:T(4,128)(2,1)}), bf16[128,4,128]{2,1,0:T(4,128)(2,1)S(1)}, u32[]{:S(2)}, u32[]{:S(2)}) %all-to-all-start) | async-done | bytes 131104 | tf_op jit(solution)/shard_map/all_to_all | solution.py:63
  94.2 0.1 copy.46
  94.3 0.2 convolution_convert_fusion
  94.6 0.8 copy.50
  95.3 2.6 %all-to-all-start.2 = ((bf16[4,128,128]{2,0,1:T(4,128)(2,1)}), bf16[4,128,128]{2,0,1:T(4,128)(2,1)S(1)}, u32[]{:S(2)}, u32[]{:S(2)}) async-start(bf16[4,128,128]{2,0,1:T(4,128)(2,1)} %copy.50), calls=%async_computation.2 | async-start | bytes 262144 | tf_op jit(solution)/shard_map/all_to_all | solution.py:67
  97.9 0.0 copy-done.6
  97.9 0.0 copy-start.4
  97.9 0.3 fusion.4
  98.2 7.9 %all-to-all-done.2 = bf16[4,128,128]{2,0,1:T(4,128)(2,1)S(1)} async-done(((bf16[4,128,128]{2,0,1:T(4,128)(2,1)}), bf16[4,128,128]{2,0,1:T(4,128)(2,1)S(1)}, u32[]{:S(2)}, u32[]{:S(2)}) %all-to-all-start.2) | async-done | bytes 131104 | tf_op jit(solution)/shard_map/all_to_all | solution.py:67
  106.1 0.1 bitcast_reduce_fusion
  106.2 0.1 fusion.25
  106.3 0.0 copy-done.4
  106.4 0.2 fusion.5
  106.6 0.8 copy.54
  (11 shorter events, 0.2 us)
Async XLA Ops:
  6.5 63.0 %copy-start = (bf16[1024,128]{1,0:T(8,128)(2,1)S(1)}, bf16[1024,128]{1,0:T(8,128)(2,1)}, u32[]{:S(2)}) copy-start(bf16[1024,128]{1,0:T(8,128)(2,1)} %param.12) | copy-start | bytes 786436
  6.5 2.7 %copy-start.1 = (bf16[128,4,256]{2,1,0:T(4,128)(2,1)S(1)}, bf16[128,4,256]{2,1,0:T(4,128)(2,1)}, u32[]{:S(2)}) copy-start(bf16[128,4,256]{2,1,0:T(4,128)(2,1)} %param.8) | copy-start | bytes 786436
  6.5 3.0 %copy-start.7 = (bf16[256,32]{0,1:T(8,128)(2,1)S(1)}, bf16[256,32]{0,1:T(8,128)(2,1)}, u32[]{:S(2)}) copy-start(bf16[256,32]{0,1:T(8,128)(2,1)} %param.11) | copy-start | bytes 49156
  6.5 3.9 %copy-start.2 = (bf16[4,128,128]{2,1,0:T(8,128)(2,1)S(1)}, bf16[4,128,128]{2,1,0:T(8,128)(2,1)}, u32[]{:S(2)}) copy-start(bf16[4,128,128]{2,1,0:T(8,128)(2,1)} %param.9) | copy-start | bytes 393220
  6.5 60.3 %all-gather.2.cloned.1.call-start = ((), (), s32[]{:S(2)}) async-start(), calls=%async_computation.3 | async-start | bytes 1081344 | tf_op jit(solution)/shard_map/all_gather | solution.py:45
  7.8 59.1 %copy-start.5 = (bf16[256,32]{0,1:T(8,128)(2,1)S(1)}, bf16[256,32]{0,1:T(8,128)(2,1)}, u32[]{:S(2)}) copy-start(bf16[256,32]{0,1:T(8,128)(2,1)} %param.10) | copy-start | bytes 49156
  69.5 0.9 copy-start.3
  71.6 11.8 %all-to-all-start.1 = ((bf16[128,4,128]{2,1,0:T(4,128)(2,1)}), bf16[128,4,128]{2,1,0:T(4,128)(2,1)S(1)}, u32[]{:S(2)}, u32[]{:S(2)}) async-start(bf16[128,4,128]{2,1,0:T(4,128)(2,1)} %copy.47), calls=%async_computation.1 | async-start | bytes 262144 | tf_op jit(solution)/shard_map/all_to_all | solution.py:64
  83.4 10.8 %all-to-all-start = ((bf16[128,4,128]{2,1,0:T(4,128)(2,1)}), bf16[128,4,128]{2,1,0:T(4,128)(2,1)S(1)}, u32[]{:S(2)}, u32[]{:S(2)}) async-start(bf16[128,4,128]{2,1,0:T(4,128)(2,1)} %copy.44), calls=%async_computation | async-start | bytes 262144 | tf_op jit(solution)/shard_map/all_to_all | solution.py:63
  86.0 11.9 %copy-start.6 = (bf16[128,128]{1,0:T(8,128)(2,1)S(1)}, bf16[128,128]{1,0:T(8,128)(2,1)}, u32[]{:S(2)}) copy-start(bf16[128,128]{1,0:T(8,128)(2,1)} %param.14) | copy-start | bytes 98308
  95.3 10.8 %all-to-all-start.2 = ((bf16[4,128,128]{2,0,1:T(4,128)(2,1)}), bf16[4,128,128]{2,0,1:T(4,128)(2,1)S(1)}, u32[]{:S(2)}, u32[]{:S(2)}) async-start(bf16[4,128,128]{2,0,1:T(4,128)(2,1)} %copy.50), calls=%async_computation.2 | async-start | bytes 262144 | tf_op jit(solution)/shard_map/all_to_all | solution.py:67
  97.9 8.4 %copy-start.4 = (bf16[128,128]{1,0:T(8,128)(2,1)S(1)}, bf16[128,128]{1,0:T(8,128)(2,1)}, u32[]{:S(2)}) copy-start(bf16[128,128]{1,0:T(8,128)(2,1)} %param.15) | copy-start | bytes 98308
Sparse Core Ops, SparseCore 0:
  10.5 56.3 all-gather.1
where the time goes:
time: 115 us; the launch traced here: 114 us
  waiting for transfers between devices  79.7 us (69%)
  between operations  13.7 us (12%)
  starting transfers between devices  8.77 us (8%)
  local copies, waits for them, and re-layouts  4.68 us (4%)
  matrix products  4.1 us (4%)
  other arithmetic  3.28 us (3%)
    all_gather x1, waiting for transfers between devices, per_device(): right_all = lax.all_gather(second_operand, 'dap', axis=1, tiled=True)  56.3 us
    all_to_all x1, waiting for transfers between devices, per_device(): lax.all_to_all(left_t, 'dap', split_axis=0, concat_axis=1, tiled=True)  8.05 us
    all_to_all x1, waiting for transfers between devices, per_device(): lax.all_to_all(product.astype(jnp.bfloat16), 'dap', split_axis=1, concat_...  7.91 us
    all_to_all x1, waiting for transfers between devices, per_device(): lax.all_to_all(right_t, 'dap', split_axis=0, concat_axis=1, tiled=True)  7.41 us
    all_to_all x1, starting transfers between devices, per_device(): lax.all_to_all(right_t, 'dap', split_axis=0, concat_axis=1, tiled=True)  3.58 us
    all_to_all x1, starting transfers between devices, per_device(): lax.all_to_all(left_t, 'dap', split_axis=0, concat_axis=1, tiled=True)  2.58 us
    all_to_all x1, starting transfers between devices, per_device(): lax.all_to_all(product.astype(jnp.bfloat16), 'dap', split_axis=1, concat_...  2.58 us
  transfers between devices with their start and end apart: 4, of which 4 were waited for; matrix products, arithmetic and copies ran while one was open for 1% of the time, Pallas kernels for 0%

commit v1 on v0

--- a/solution.py
+++ b/solution.py
@@ -1,7 +1,18 @@
+import functools
 import jax
 import jax.numpy as jnp
 from jax import lax
 from jax.sharding import PartitionSpec as P
+
+
+def _derive_classes(inner_x, array_axis, row_dim):
+    return jnp.concatenate(
+        lax.all_to_all(jnp.stack(jnp.split(inner_x, lax.axis_size("dap"), row_dim)), "dap", 0, 0),
+        array_axis,
+    )
+
+
+_convert_matrix = functools.partial(_derive_classes, array_axis=1, row_dim=0)
 
 
 def standardize_fn(value, axis):
@@ -61,7 +72,7 @@
     right_t = (jax.nn.sigmoid(projected[2]) * projected[3]).astype(jnp.bfloat16)
     left_cols, right_cols = (
         lax.all_to_all(left_t, "dap", split_axis=0, concat_axis=1, tiled=True),
-        lax.all_to_all(right_t, "dap", split_axis=0, concat_axis=1, tiled=True),
+        _convert_matrix(right_t),
     )
     product = jnp.einsum("cik,cjk->cij", left_cols, right_cols, preferred_element_type=jnp.float32)
     returned = lax.all_to_all(

time: 115 us -> 114 us (level)
  no operation moved by 1% of the time
where the time goes in v1:
time: 114 us
  waiting for transfers between devices  79.3 us (70%)
  between operations  13.8 us (12%)
  starting transfers between devices  8.75 us (8%)
  local copies, waits for them, and re-layouts  4.83 us (4%)
  matrix products  4.11 us (4%)
  other arithmetic  3.28 us (3%)
    all_gather x1, waiting for transfers between devices, per_device(): right_all = lax.all_gather(second_operand, 'dap', axis=1, tiled=True)  56.3 us
    all_to_all x1, waiting for transfers between devices, _derive_classes(): lax.all_to_all(jnp.stack(jnp.split(inner_x, lax.axis_size('dap'), row_dim...  8.15 us
    all_to_all x1, waiting for transfers between devices, per_device(): lax.all_to_all(product.astype(jnp.bfloat16), 'dap', split_axis=1, concat_...  7.91 us
    all_to_all x1, waiting for transfers between devices, per_device(): lax.all_to_all(left_t, 'dap', split_axis=0, concat_axis=1, tiled=True)  6.93 us
    all_to_all x1, starting transfers between devices, per_device(): lax.all_to_all(left_t, 'dap', split_axis=0, concat_axis=1, tiled=True)  3.58 us
    all_to_all x1, starting transfers between devices, per_device(): lax.all_to_all(product.astype(jnp.bfloat16), 'dap', split_axis=1, concat_...  2.58 us
    all_to_all x1, starting transfers between devices, _derive_classes(): lax.all_to_all(jnp.stack(jnp.split(inner_x, lax.axis_size('dap'), row_dim...  2.56 us
  transfers between devices with their start and end apart: 4, of which 4 were waited for; matrix products, arithmetic and copies ran while one was open for 1% of the time, Pallas kernels for 0%

profile of v1, /device:TPU:0, one launch (start us, length us, event | category | flops | bytes accessed | tf_op | source)
XLA Modules:
  0.0 114.1 jit_solution(2523740966811021534)
XLA Ops:
  6.5 0.0 copy-start
  6.5 0.0 copy-start.1
  6.5 0.0 copy-start.7
  6.5 0.0 copy-start.2
  6.5 0.0 all-gather.2.cloned.1.call-start
  6.6 1.2 %convert_reduce_fusion = f32[128,4]{1,0:T(8,128)S(1)} fusion(bf16[128,4,256]{2,1,0:T(4,128)(2,1)} %param.8), kind=kLoop, calls=%fused_computation.21 | loop fusion | flops 261632 | bytes 264192 | tf_op jit(solution)/shard_map/reduce_sum | solution.py:19
  7.8 0.0 copy-start.5
  7.8 1.3 %fusion.14 = f32[128,4]{1,0:T(8,128)S(1)} fusion(bf16[128,4,256]{2,1,0:T(4,128)(2,1)} %param.8, f32[128,4]{1,0:T(8,128)S(1)} %broadcast_multiply_fusion), kind=kLoop, calls=%fused_computation.24 | loop fusion | flops 523776 | bytes 266240 | tf_op jit(solution)/shard_map/reduce_sum | solution.py:21
  9.2 0.0 copy-done.1
  9.2 0.3 fusion.15
  9.6 0.0 copy-done.7
  9.6 0.8 convolution_convert_fusion.3
  10.4 0.0 all-gather.2.cloned.1.call-update
  10.4 0.0 copy-done.2
  10.4 0.1 copy.33
  10.5 56.3 %all-gather.2.cloned.1.call-done = bf16[128,128,32]{0,2,1:T(8,128)(2,1)} async-done(((bf16[128,4,32]{0,2,1:T(8,128)(2,1)}), bf16[128,128,32]{0,2,1:T(8,128)(2,1)}) %all-gather.2.cloned.1.call-update) | async-done | bytes 1048592 | tf_op jit(solution)/shard_map/all_gather | solution.py:56
  66.9 0.0 copy-done.5
  66.9 1.9 %fusion = bf16[4,128,32,32]{1,2,0,3:T(8,128)(2,1)S(1)} fusion(bf16[128,128,32,1]{0,2,1,3:T(8,128)(2,1)} %bitcast.61, bf16[128,4,256]{2,1,0:T(4,128)(2,1)S(1)} %fusion.15, bf16[256,32]{0,1:T(8,128)(2,1)S(1)} %copy-done.5), kind=kOutput, calls=%fused_computation.1 | convolution fusion | flops 143671296 | bytes 2375680 | tf_op jit(solution)/shard_map/sic,sje->ijce/dot_general | solution.py:27
  68.8 0.7 copy.37
  69.5 0.0 copy-start.3
  69.5 0.0 copy-done
  69.5 0.4 fusion.40
  69.9 0.5 copy-done.3
  70.4 0.3 convolution_bitcast_fusion
  70.7 0.1 fusion.16
  70.9 0.8 copy.44
  71.6 3.6 %all-to-all-start = ((bf16[128,4,128]{2,1,0:T(4,128)(2,1)}), bf16[128,4,128]{2,1,0:T(4,128)(2,1)S(1)}, u32[]{:S(2)}, u32[]{:S(2)}) async-start(bf16[128,4,128]{2,1,0:T(4,128)(2,1)} %copy.44), calls=%async_computation | async-start | bytes 262144 | tf_op jit(solution)/shard_map/all_to_all | solution.py:74
  75.5 0.0 copy-start.6
  75.8 0.7 copy.46
  76.5 6.9 %all-to-all-done = bf16[128,4,128]{2,1,0:T(4,128)(2,1)S(1)} async-done(((bf16[128,4,128]{2,1,0:T(4,128)(2,1)}), bf16[128,4,128]{2,1,0:T(4,128)(2,1)S(1)}, u32[]{:S(2)}, u32[]{:S(2)}) %all-to-all-start) | async-done | bytes 131104 | tf_op jit(solution)/shard_map/all_to_all | solution.py:74
  83.4 2.6 %all-to-all-start.1 = ((bf16[32,4,4,128]{3,1,2,0:T(4,128)(2,1)}), bf16[32,4,4,128]{3,1,2,0:T(4,128)(2,1)S(1)}, u32[]{:S(2)}, u32[]{:S(2)}) async-start(bf16[32,4,4,128]{3,1,2,0:T(4,128)(2,1)} %copy.46), calls=%async_computation.1 | async-start | bytes 262144 | tf_op jit(solution)/shard_map/all_to_all | solution.py:10
  86.1 8.1 %all-to-all-done.1 = bf16[32,4,4,128]{3,1,2,0:T(4,128)(2,1)S(1)} async-done(((bf16[32,4,4,128]{3,1,2,0:T(4,128)(2,1)}), bf16[32,4,4,128]{3,1,2,0:T(4,128)(2,1)S(1)}, u32[]{:S(2)}, u32[]{:S(2)}) %all-to-all-start.1) | async-done | bytes 131104 | tf_op jit(solution)/shard_map/all_to_all | solution.py:10
  94.2 0.1 copy.47
  94.3 0.2 convolution_convert_fusion
  94.5 0.8 copy.48
  95.2 2.6 %all-to-all-start.2 = ((bf16[4,128,128]{2,0,1:T(4,128)(2,1)}), bf16[4,128,128]{2,0,1:T(4,128)(2,1)S(1)}, u32[]{:S(2)}, u32[]{:S(2)}) async-start(bf16[4,128,128]{2,0,1:T(4,128)(2,1)} %copy.48), calls=%async_computation.2 | async-start | bytes 262144 | tf_op jit(solution)/shard_map/all_to_all | solution.py:78
  97.8 0.0 copy-done.6
  97.8 0.0 copy-start.4
  97.8 0.3 fusion.4
  98.1 7.9 %all-to-all-done.2 = bf16[4,128,128]{2,0,1:T(4,128)(2,1)S(1)} async-done(((bf16[4,128,128]{2,0,1:T(4,128)(2,1)}), bf16[4,128,128]{2,0,1:T(4,128)(2,1)S(1)}, u32[]{:S(2)}, u32[]{:S(2)}) %all-to-all-start.2) | async-done | bytes 131104 | tf_op jit(solution)/shard_map/all_to_all | solution.py:78
  106.0 0.1 bitcast_reduce_fusion
  106.1 0.1 fusion.25
  106.3 0.0 copy-done.4
  106.3 0.2 fusion.5
  106.5 0.8 copy.52
  (42 shorter events, 0.6 us)
Async XLA Ops:
  6.5 63.0 %copy-start = (bf16[1024,128]{1,0:T(8,128)(2,1)S(1)}, bf16[1024,128]{1,0:T(8,128)(2,1)}, u32[]{:S(2)}) copy-start(bf16[1024,128]{1,0:T(8,128)(2,1)} %param.12) | copy-start | bytes 786436
  6.5 2.7 %copy-start.1 = (bf16[128,4,256]{2,1,0:T(4,128)(2,1)S(1)}, bf16[128,4,256]{2,1,0:T(4,128)(2,1)}, u32[]{:S(2)}) copy-start(bf16[128,4,256]{2,1,0:T(4,128)(2,1)} %param.8) | copy-start | bytes 786436
  6.5 3.0 %copy-start.7 = (bf16[256,32]{0,1:T(8,128)(2,1)S(1)}, bf16[256,32]{0,1:T(8,128)(2,1)}, u32[]{:S(2)}) copy-start(bf16[256,32]{0,1:T(8,128)(2,1)} %param.11) | copy-start | bytes 49156
  6.5 3.9 %copy-start.2 = (bf16[4,128,128]{2,1,0:T(8,128)(2,1)S(1)}, bf16[4,128,128]{2,1,0:T(8,128)(2,1)}, u32[]{:S(2)}) copy-start(bf16[4,128,128]{2,1,0:T(8,128)(2,1)} %param.9) | copy-start | bytes 393220
  6.5 60.3 %all-gather.2.cloned.1.call-start = ((), (), s32[]{:S(2)}) async-start(), calls=%async_computation.3 | async-start | bytes 1081344 | tf_op jit(solution)/shard_map/all_gather | solution.py:56
  7.8 59.1 %copy-start.5 = (bf16[256,32]{0,1:T(8,128)(2,1)S(1)}, bf16[256,32]{0,1:T(8,128)(2,1)}, u32[]{:S(2)}) copy-start(bf16[256,32]{0,1:T(8,128)(2,1)} %param.10) | copy-start | bytes 49156
  69.5 0.9 copy-start.3
  71.6 11.8 %all-to-all-start = ((bf16[128,4,128]{2,1,0:T(4,128)(2,1)}), bf16[128,4,128]{2,1,0:T(4,128)(2,1)S(1)}, u32[]{:S(2)}, u32[]{:S(2)}) async-start(bf16[128,4,128]{2,1,0:T(4,128)(2,1)} %copy.44), calls=%async_computation | async-start | bytes 262144 | tf_op jit(solution)/shard_map/all_to_all | solution.py:74
  75.5 22.3 %copy-start.6 = (bf16[128,128]{1,0:T(8,128)(2,1)S(1)}, bf16[128,128]{1,0:T(8,128)(2,1)}, u32[]{:S(2)}) copy-start(bf16[128,128]{1,0:T(8,128)(2,1)} %param.14) | copy-start | bytes 98308
  83.4 10.8 %all-to-all-start.1 = ((bf16[32,4,4,128]{3,1,2,0:T(4,128)(2,1)}), bf16[32,4,4,128]{3,1,2,0:T(4,128)(2,1)S(1)}, u32[]{:S(2)}, u32[]{:S(2)}) async-start(bf16[32,4,4,128]{3,1,2,0:T(4,128)(2,1)} %copy.46), calls=%async_computation.1 | async-start | bytes 262144 | tf_op jit(solution)/shard_map/all_to_all | solution.py:10
  95.2 10.8 %all-to-all-start.2 = ((bf16[4,128,128]{2,0,1:T(4,128)(2,1)}), bf16[4,128,128]{2,0,1:T(4,128)(2,1)S(1)}, u32[]{:S(2)}, u32[]{:S(2)}) async-start(bf16[4,128,128]{2,0,1:T(4,128)(2,1)} %copy.48), calls=%async_computation.2 | async-start | bytes 262144 | tf_op jit(solution)/shard_map/all_to_all | solution.py:78
  97.8 8.4 %copy-start.4 = (bf16[128,128]{1,0:T(8,128)(2,1)S(1)}, bf16[128,128]{1,0:T(8,128)(2,1)}, u32[]{:S(2)}) copy-start(bf16[128,128]{1,0:T(8,128)(2,1)} %param.15) | copy-start | bytes 98308
Sparse Core Ops, SparseCore 0:
  10.5 56.3 all-gather.1
